TPU v7x, 32 devices: a whole 2x2x4 slice. The times are simulated.
32 devices in a mesh: dp: 8 (over z, x), rep: 4 (over y, core).
Axes of the slice: x: 2, y: 2, z: 4, core: 2. Of those that a mesh axis runs over, the one named last changes fastest.
Arguments:
- features: bfloat16 [5120, 8192], P('dp', 'rep'), may hold values from -6 to 6
- out_grads: bfloat16 [5120, 1024], P('dp'), may hold values from -12 to 12, as said below
- cold_sums: bfloat16 [8, 8192, 1024], P('dp', 'rep'), may hold values from -96 to 96
- weight: float32 [8192, 1024], P(('rep', 'dp')), may hold values from -3 to 3
- moment: float32 [8192, 1024], P(('rep', 'dp')), may hold values from -6 to 6
- second: float32 [8192, 1024], P(('rep', 'dp')), may hold values from 0.01 to 4
- ranks: int32 [8], replicated, may hold values from 0 to 7, each once
Outputs:
- new_weight: float32 [8192, 1024], P(('rep', 'dp'))
- new_moment: float32 [8192, 1024], P(('rep', 'dp'))
- new_second: float32 [8192, 1024], P(('rep', 'dp'))
- new_cold: bfloat16 [8, 8192, 1024], P('dp', 'rep')
- column_sq: float32 [1024], replicated
Inputs may be any that keep to these rules, and one draw needn't show every extreme that they name: `ranks`: each block number appears once. `out_grads`: column scales differ from column to column.
All inputs are finite; a program needn't handle non-finite values.
Results may differ from a plain program's by a relative error of at most 0.001.
Values sent between devices are 32-bit elements; how exact they have to be, the bound alone decides.
No kernel may reach another device: no remote copies, remote signals or barrier semaphores. Data moves between devices by JAX's collectives and lax.ppermute only.
A program may use at most 128 MiB of HBM per device.

v0:
```python
import jax
import jax.numpy as jnp
from jax import lax
from jax.sharding import PartitionSpec as P


def cycle(count):
    return list(range(1, count, 2)) + list(reversed(range(0, count, 2)))


def body(features, out_grads, cold_sums, weight, moment, second, ranks):
    blocks = ranks.shape[0]
    hot_count = blocks // 2
    width = out_grads.shape[1]
    local_rows = features.shape[1]
    grad = lax.dot_general(
        features, out_grads, (((0,), (0,)), ((), ())), preferred_element_type=jnp.float32
    )
    local = cold_sums[0].astype(jnp.float32) + grad
    hot_block = ranks < hot_count
    hot_col = jnp.repeat(hot_block, 128)
    new_cold = jnp.where(hot_col[None, :], jnp.float32(0.0), local).astype(jnp.bfloat16)[None]
    partial_sq = jnp.sum(local * local, axis=0)
    column_sq = lax.psum(partial_sq, ("dp", "rep"))
    picker = (ranks[None, :] == jnp.arange(hot_count, dtype=jnp.int32)[:, None]).astype(jnp.float32)
    packed = jnp.einsum(
        "rbk,sb->rsk",
        local.reshape(local_rows, blocks, 128),
        picker,
        precision=lax.Precision.HIGHEST,
    )
    members = cycle(lax.axis_size("dp"))
    part = packed.reshape(len(members), local_rows // len(members), hot_count * 128)
    ordered = jnp.concatenate([part[m] for m in members], axis=0)
    owned = lax.psum_scatter(
        ordered, "dp", scatter_dimension=0, tiled=True, axis_index_groups=[members]
    )
    owned_rows = owned.shape[0]
    spread = jnp.einsum(
        "rsk,sb->rbk",
        owned.reshape(owned_rows, hot_count, 128),
        picker,
        precision=lax.Precision.HIGHEST,
    )
    summed = spread.reshape(owned_rows, width)
    dp_count = lax.axis_size("dp")
    total_rows = local_rows * lax.axis_size("rep")
    rms = jnp.sqrt(column_sq / jnp.float32(total_rows * dp_count * features.shape[0]))
    clip = 1.0 / jnp.maximum(jnp.float32(1.0), rms)
    grad_mean = summed * clip[None, :] / jnp.float32(dp_count)
    moved = 0.9 * moment + 0.1 * grad_mean
    squared = 0.95 * second + 0.05 * grad_mean * grad_mean
    step_size = 0.05 * (moved / (1.0 - 0.9**10)) / (jnp.sqrt(squared / (1.0 - 0.95**10)) + 1e-08)
    new_moment = jnp.where(hot_col[None, :], moved, moment)
    new_second = jnp.where(hot_col[None, :], squared, second)
    new_weight = jnp.where(hot_col[None, :], weight - step_size, weight)
    return (new_weight, new_moment, new_second, new_cold, column_sq)


def solution(mesh):
    placed = (
        P("dp", "rep"),
        P("dp", None),
        P("dp", "rep", None),
        P(("rep", "dp"), None),
        P(("rep", "dp"), None),
        P(("rep", "dp"), None),
        P(),
    )
    return jax.shard_map(
        body,
        mesh=mesh,
        in_specs=placed,
        out_specs=(
            P(("rep", "dp"), None),
            P(("rep", "dp"), None),
            P(("rep", "dp"), None),
            P("dp", "rep", None),
            P(),
        ),
        check_vma=False,
    )
```

profile of v0, /device:TPU:0, one launch (start us, length us, event | category | flops | bytes accessed | tf_op | source)
XLA Modules:
  0.0 115.6 jit_solution(7516741653848244742)
XLA Ops:
  7.2 0.0 copy-start
  7.2 0.0 reduce-scatter.2.cloned.1.call-start
  7.2 6.6 %copy.12 = bf16[1,2048,1024]{1,2,0:T(8,128)(2,1)} copy(bf16[1,2048,1024]{2,1,0:T(8,128)(2,1)} %param.9) | data formatting | bytes 8388608 | tf_op args[2]
  13.8 0.0 copy-done
  13.8 8.2 %multiply_reduce_fusion = (f32[1024]{0:T(1024)S(1)}, f32[2048,1024]{0,1:T(8,128)}) fusion(bf16[640,2048]{1,0:T(8,128)(2,1)S(1)} %copy-done, bf16[640,1024]{1,0:T(8,128)(2,1)} %param.8, bf16[1,2048,1024]{1,2,0:T(8,128)(2,1)} %copy.12), kind=kOutput, calls=%fused_computation.2 | convolution fusion | flops 2692742144 | bytes 16519168 | tf_op jit(solution)/shard_map/dot_general | solution.py:16
  22.0 0.0 copy-start.2
  22.0 9.3 %copy.13 = f32[2048,8,128]{2,1,0:T(8,128)} copy(f32[2048,8,128]{0,2,1:T(8,128)} %bitcast.58) | data formatting | bytes 16777216 | tf_op jit(solution)/shard_map/reshape | solution.py:28
  31.3 0.0 copy-done.2
  31.3 7.4 %convolution_bitcast_fusion = f32[2048,4,128]{2,1,0:T(4,128)S(1)} fusion(f32[2048,8,128]{2,1,0:T(8,128)} %copy.13, s32[8]{0:T(128)S(1)} %copy-done.2), kind=kOutput, calls=%fused_computation.4 | convolution fusion | flops 100663328 | bytes 12582944 | tf_op jit(solution)/shard_map/rbk,sb->rsk/dot_general | solution.py:26
  38.7 0.3 fusion.9
  39.0 0.9 bitcast_dynamic-update-slice_fusion.7
  39.8 0.9 bitcast_dynamic-update-slice_fusion.6
  40.7 0.8 bitcast_dynamic-update-slice_fusion.5
  41.6 0.8 bitcast_dynamic-update-slice_fusion.4
  42.4 0.9 bitcast_dynamic-update-slice_fusion.3
  43.3 0.8 bitcast_dynamic-update-slice_fusion.2
  44.1 0.8 bitcast_dynamic-update-slice_fusion.1
  44.9 0.8 bitcast_dynamic-update-slice_fusion
  45.8 0.0 reduce-scatter.2.cloned.1.call-update
  45.8 0.1 broadcast_bitcast_fusion
  45.9 5.9 %fusion = bf16[1,2048,1024]{1,2,0:T(8,128)(2,1)} fusion(f32[2048,1024]{0,1:T(8,128)} %get-tuple-element.22, pred[1024]{0:T(1024)(128)(4,1)S(1)} %broadcast_bitcast_fusion), kind=kLoop, calls=%fused_computation.3 | loop fusion | flops 2097152 | bytes 12583936 | tf_op jit(solution)/shard_map/broadcast_in_dim | solution.py:22
  51.8 6.3 %copy.14 = bf16[1,2048,1024]{2,1,0:T(8,128)(2,1)} copy(bf16[1,2048,1024]{1,2,0:T(8,128)(2,1)} %fusion) | data formatting | bytes 8388608
  58.1 44.1 %psum.7 = f32[1024]{0:T(1024)S(1)} all-reduce(f32[1024]{0:T(1024)S(1)} %get-tuple-element.21), channel_id=1, replica_groups=mesh['dp'=8,'rep'=4] {'dp','rep'}, use_global_device_ids=true, to_apply=%region_2.3 | all-reduce | flops 1024 | bytes 8192 | tf_op jit(solution)/shard_map/psum | solution.py:24
  102.1 0.0 copy-start.1
  102.1 0.0 reduce-scatter.2.cloned.1.call-done
  102.1 1.2 %reshape.42 = f32[256,4,128]{2,1,0:T(4,128)S(1)} reshape(f32[256,512]{1,0:T(8,128)} %reduce-scatter.2.cloned.1.call-done) | data formatting | bytes 1048576 | tf_op jit(solution)/shard_map/reshape | solution.py:41
  103.4 0.7 fusion.4
  104.1 4.6 %fusion.2 = (f32[256,1024]{1,0:T(8,128)}, f32[256,1024]{1,0:T(8,128)}, f32[256,1024]{1,0:T(8,128)}) fusion(f32[256,1024]{1,0:T(8,128)} %param.12, f32[32,8,8,128]{3,2,1,0:T(8,128)S(1)} %bitcast.59, f32[1024]{0:T(1024)S(1)} %maximum_divide_fusion, pred[1024]{0:T(1024)(128)(4,1)S(1)} %broadcast_bitcast_fusion, f32[256,1024]{1,0:T(8,128)} %param.10, ...), kind=kLoop, calls=%fused_computation.10 | loop fusion | flops 4456448 | bytes 7345152 | tf_op jit(solution)/shard_map/jit(_where)/select_n | solution.py:55
  108.7 0.0 copy-done.1
  (2 shorter events, 0.0 us)
Async XLA Ops:
  7.2 6.6 %copy-start = (bf16[640,2048]{1,0:T(8,128)(2,1)S(1)}, bf16[640,2048]{1,0:T(8,128)(2,1)}, u32[]{:S(2)}) copy-start(bf16[640,2048]{1,0:T(8,128)(2,1)} %param.7) | copy-start | bytes 7864324
  7.2 95.0 %reduce-scatter.2.cloned.1.call-start = ((), (), s32[]{:S(2)}) async-start(), calls=%async_computation.1 | async-start | bytes 4718592 | tf_op jit(solution)/shard_map/reduce_scatter | solution.py:35
  22.0 9.3 %copy-start.2 = (s32[8]{0:T(128)S(1)}, s32[8]{0:T(128)}, u32[]{:S(2)}) copy-start(s32[8]{0:T(128)} %param.13) | copy-start | bytes 100
  102.1 6.6 %copy-start.1 = (f32[1024]{0:T(1024)}, f32[1024]{0:T(1024)S(1)}, u32[]{:S(2)}) copy-start(f32[1024]{0:T(1024)S(1)} %psum.7) | copy-start | bytes 12292
Sparse Core Ops, SparseCore 0:
  45.9 52.1 reduce-scatter.1
where the time goes:
time: 116 us
  blocking collectives  44.1 us (38%)
  local copies, waits for them, and re-layouts  30.5 us (26%)
  matrix products  16.3 us (14%)
  between operations  14.1 us (12%)
  other arithmetic  10.5 us (9%)
    psum x1, blocking collectives, body(): column_sq = lax.psum(partial_sq, ('dp', 'rep'))  44.1 us
    unnamed x15, local copies, waits for them, and re-layouts  18.8 us
    reshape x1, local copies, waits for them, and re-layouts, body(): local.reshape(local_rows, blocks, 128)  9.29 us
    dot_general x1, matrix products, body(): lax.dot_general(features, out_grads, (((0,), (0,)), ((), ())), preferred_...  8.15 us
    dot_general x1, matrix products, body(): jnp.einsum('rbk,sb->rsk', local.reshape(local_rows, blocks, 128), picker,...  7.42 us
    broadcast_in_dim x1, other arithmetic, body(): jnp.where(hot_col[None, :], jnp.float32(0.0), local).astype(jnp.bfloat16)  5.87 us
    select_n x1, other arithmetic, body(): new_second = jnp.where(hot_col[None, :], squared, second)  4.64 us
  transfers between devices with their start and end apart: 1, of which 0 were waited for; matrix products, arithmetic and copies ran while one was open for 11% of the time, Pallas kernels for 0%

commit v1 on v0

--- a/solution.py
+++ b/solution.py
@@ -21,7 +21,7 @@
     hot_col = jnp.repeat(hot_block, 128)
     new_cold = jnp.where(hot_col[None, :], jnp.float32(0.0), local).astype(jnp.bfloat16)[None]
     partial_sq = jnp.sum(local * local, axis=0)
-    column_sq = lax.psum(partial_sq, ("dp", "rep"))
+    column_sq = lax.psum(lax.psum(partial_sq, "rep"), "dp")
     picker = (ranks[None, :] == jnp.arange(hot_count, dtype=jnp.int32)[:, None]).astype(jnp.float32)
     packed = jnp.einsum(
         "rbk,sb->rsk",

time: 116 us -> 112 us (0.966)
  blocking collectives: 44.1 us -> 31.1 us
  waiting for transfers between devices: 0.04 us -> 8.55 us
    psum x1 -> x2, blocking collectives: 44.1 us -> 31.1 us  [body(): column_sq = lax.psum(lax.psum(partial_sq, 'rep'), 'dp')]
    reduce_scatter x1, waiting for transfers between devices: 0.02 us -> 8.54 us  [body(): lax.psum_scatter(ordered, 'dp', scatter_dimension=0, tiled=True, axis_ind...]
  transfers between devices with their start and end apart: 1 -> 1, of which waited for: 0 -> 1; matrix products, arithmetic and copies ran while one was open for 11% -> 11% of each run, Pallas kernels for 0% -> 0%
where the time goes in v1:
time: 112 us; the launch traced here: 111 us
  blocking collectives  31.1 us (28%)
  local copies, waits for them, and re-layouts  30.6 us (27%)
  matrix products  16.2 us (14%)
  between operations  14.1 us (13%)
  other arithmetic  10.5 us (9%)
  waiting for transfers between devices  8.55 us (8%)
    psum x2, blocking collectives, body(): column_sq = lax.psum(lax.psum(partial_sq, 'rep'), 'dp')  31.1 us
    unnamed x15, local copies, waits for them, and re-layouts  18.9 us
    reshape x1, local copies, waits for them, and re-layouts, body(): local.reshape(local_rows, blocks, 128)  9.3 us
    reduce_scatter x1, waiting for transfers between devices, body(): lax.psum_scatter(ordered, 'dp', scatter_dimension=0, tiled=True, axis_ind...  8.54 us
    dot_general x1, matrix products, body(): lax.dot_general(features, out_grads, (((0,), (0,)), ((), ())), preferred_...  8.02 us
    dot_general x1, matrix products, body(): jnp.einsum('rbk,sb->rsk', local.reshape(local_rows, blocks, 128), picker,...  7.42 us
    broadcast_in_dim x1, other arithmetic, body(): jnp.where(hot_col[None, :], jnp.float32(0.0), local).astype(jnp.bfloat16)  5.88 us
    select_n x1, other arithmetic, body(): new_second = jnp.where(hot_col[None, :], squared, second)  4.64 us
  transfers between devices with their start and end apart: 1, of which 1 were waited for; matrix products, arithmetic and copies ran while one was open for 11% of the time, Pallas kernels for 0%

profile of v1, /device:TPU:0, one launch (start us, length us, event | category | flops | bytes accessed | tf_op | source)
XLA Modules:
  0.0 111.0 jit_solution(15563694525048485234)
XLA Ops:
  7.2 0.0 copy-start
  7.2 0.0 reduce-scatter.2.cloned.1.call-start
  7.2 6.6 %copy.12 = bf16[1,2048,1024]{1,2,0:T(8,128)(2,1)} copy(bf16[1,2048,1024]{2,1,0:T(8,128)(2,1)} %param.9) | data formatting | bytes 8388608 | tf_op args[2]
  13.8 0.0 copy-done
  13.8 8.0 %multiply_reduce_fusion = (f32[1024]{0:T(1024)S(1)}, f32[2048,1024]{0,1:T(8,128)}) fusion(bf16[640,2048]{1,0:T(8,128)(2,1)S(1)} %copy-done, bf16[640,1024]{1,0:T(8,128)(2,1)} %param.8, bf16[1,2048,1024]{1,2,0:T(8,128)(2,1)} %copy.12), kind=kOutput, calls=%fused_computation.2 | convolution fusion | flops 2692742144 | bytes 16519168 | tf_op jit(solution)/shard_map/dot_general | solution.py:16
  21.8 0.0 copy-start.2
  21.8 9.3 %copy.13 = f32[2048,8,128]{2,1,0:T(8,128)} copy(f32[2048,8,128]{0,2,1:T(8,128)} %bitcast.58) | data formatting | bytes 16777216 | tf_op jit(solution)/shard_map/reshape | solution.py:28
  31.1 0.0 copy-done.2
  31.1 7.4 %convolution_bitcast_fusion = f32[2048,4,128]{2,1,0:T(4,128)S(1)} fusion(f32[2048,8,128]{2,1,0:T(8,128)} %copy.13, s32[8]{0:T(128)S(1)} %copy-done.2), kind=kOutput, calls=%fused_computation.4 | convolution fusion | flops 100663328 | bytes 12582944 | tf_op jit(solution)/shard_map/rbk,sb->rsk/dot_general | solution.py:26
  38.6 0.3 fusion.9
  38.8 0.9 bitcast_dynamic-update-slice_fusion.7
  39.7 0.9 bitcast_dynamic-update-slice_fusion.6
  40.6 0.8 bitcast_dynamic-update-slice_fusion.5
  41.5 0.8 bitcast_dynamic-update-slice_fusion.4
  42.3 0.9 bitcast_dynamic-update-slice_fusion.3
  43.1 0.8 bitcast_dynamic-update-slice_fusion.2
  44.0 0.8 bitcast_dynamic-update-slice_fusion.1
  44.8 0.8 bitcast_dynamic-update-slice_fusion
  45.7 0.0 reduce-scatter.2.cloned.1.call-update
  45.7 0.1 broadcast_bitcast_fusion
  45.8 5.9 %fusion = bf16[1,2048,1024]{1,2,0:T(8,128)(2,1)} fusion(f32[2048,1024]{0,1:T(8,128)} %get-tuple-element.22, pred[1024]{0:T(1024)(128)(4,1)S(1)} %broadcast_bitcast_fusion), kind=kLoop, calls=%fused_computation.3 | loop fusion | flops 2097152 | bytes 12583936 | tf_op jit(solution)/shard_map/broadcast_in_dim | solution.py:22
  51.6 6.3 %copy.14 = bf16[1,2048,1024]{2,1,0:T(8,128)(2,1)} copy(bf16[1,2048,1024]{1,2,0:T(8,128)(2,1)} %fusion) | data formatting | bytes 8388608
  57.9 8.6 %psum.14 = f32[1024]{0:T(1024)S(1)} all-reduce(f32[1024]{0:T(1024)S(1)} %get-tuple-element.21), channel_id=1, replica_groups=mesh['dp'=8,'rep'=4] {'rep'}, use_global_device_ids=true, to_apply=%region_2.3 | all-reduce | flops 1024 | bytes 8192 | tf_op jit(solution)/shard_map/psum | solution.py:24
  66.5 22.5 %psum.15 = f32[1024]{0:T(1024)S(1)} all-reduce(f32[1024]{0:T(1024)S(1)} %psum.14), channel_id=1, replica_groups=mesh['dp'=8,'rep'=4] {'dp'}, use_global_device_ids=true, to_apply=%region_3.4 | all-reduce | flops 1024 | bytes 8192 | tf_op jit(solution)/shard_map/psum | solution.py:24
  89.0 0.0 copy-start.1
  89.1 8.5 %reduce-scatter.2.cloned.1.call-done = f32[256,512]{1,0:T(8,128)} async-done(((f32[2048,512]{1,0:T(8,128)}), f32[256,512]{1,0:T(8,128)}) %reduce-scatter.2.cloned.1.call-update) | async-done | bytes 524304 | tf_op jit(solution)/shard_map/reduce_scatter | solution.py:35
  97.6 1.2 %reshape.42 = f32[256,4,128]{2,1,0:T(4,128)S(1)} reshape(f32[256,512]{1,0:T(8,128)} %reduce-scatter.2.cloned.1.call-done) | data formatting | bytes 1048576 | tf_op jit(solution)/shard_map/reshape | solution.py:41
  98.8 0.7 fusion.4
  99.5 4.6 %fusion.2 = (f32[256,1024]{1,0:T(8,128)}, f32[256,1024]{1,0:T(8,128)}, f32[256,1024]{1,0:T(8,128)}) fusion(f32[256,1024]{1,0:T(8,128)} %param.12, f32[32,8,8,128]{3,2,1,0:T(8,128)S(1)} %bitcast.59, f32[1024]{0:T(1024)S(1)} %maximum_divide_fusion, pred[1024]{0:T(1024)(128)(4,1)S(1)} %broadcast_bitcast_fusion, f32[256,1024]{1,0:T(8,128)} %param.10, ...), kind=kLoop, calls=%fused_computation.10 | loop fusion | flops 4456448 | bytes 7345152 | tf_op jit(solution)/shard_map/jit(_where)/select_n | solution.py:55
  104.2 0.0 copy-done.1
  (2 shorter events, 0.0 us)
Async XLA Ops:
  7.2 6.6 %copy-start = (bf16[640,2048]{1,0:T(8,128)(2,1)S(1)}, bf16[640,2048]{1,0:T(8,128)(2,1)}, u32[]{:S(2)}) copy-start(bf16[640,2048]{1,0:T(8,128)(2,1)} %param.7) | copy-start | bytes 7864324
  7.2 90.4 %reduce-scatter.2.cloned.1.call-start = ((), (), s32[]{:S(2)}) async-start(), calls=%async_computation.1 | async-start | bytes 4718592 | tf_op jit(solution)/shard_map/reduce_scatter | solution.py:35
  21.8 9.3 %copy-start.2 = (s32[8]{0:T(128)S(1)}, s32[8]{0:T(128)}, u32[]{:S(2)}) copy-start(s32[8]{0:T(128)} %param.13) | copy-start | bytes 100
  89.0 15.1 %copy-start.1 = (f32[1024]{0:T(1024)}, f32[1024]{0:T(1024)S(1)}, u32[]{:S(2)}) copy-start(f32[1024]{0:T(1024)S(1)} %psum.15) | copy-start | bytes 12292
Sparse Core Ops, SparseCore 0:
  45.8 51.7 reduce-scatter.1
